TPU v7x, 256 devices: a whole 4x4x8 slice. The times are simulated.
256 devices in a mesh: expert: 8 (over x, core), ffn: 32 (over z, y).
Axes of the slice: x: 4, y: 4, z: 8, core: 2. Of those that a mesh axis runs over, the one named last changes fastest.
Arguments:
- tokens: bfloat16 [8, 128, 4096], P('expert', 'ffn'), may hold values from -6 to 6
- routes: int32 [8, 128, 2], P('expert'), may hold values from 0 to 7, all different within a row; in each aligned block of 128 rows (0 to 127, 128 to 255, ..., all dimensions but the last counted through in order) at most 48 rows name the same one
- router: bfloat16 [4096, 8], replicated, may hold values from -0.09375 to 0.09375
- w_gate: bfloat16 [8, 4096, 12288], P('expert', None, 'ffn'), may hold values from -0.09375 to 0.09375
- w_up: bfloat16 [8, 4096, 12288], P('expert', None, 'ffn'), may hold values from -0.09375 to 0.09375
- w_down: bfloat16 [8, 12288, 4096], P('expert', 'ffn'), may hold values from -0.109375 to 0.109375
- adapter: bfloat16 [8, 4096, 4096], P('expert', None, 'ffn'), may hold values from -0.09375 to 0.09375
- upstream: bfloat16 [8, 128, 4096], P('expert', None, 'ffn'), may hold values from -24 to 24
- bound: float32 [8], P('expert'), may hold values from 2048 to 16384
Outputs:
- adapted: bfloat16 [8, 128, 4096], P('expert', None, 'ffn')
- clipped: bfloat16 [8, 4096, 4096], P('expert', None, 'ffn')
Inputs may be any that keep to these rules, and one draw needn't show every extreme that they name: `routes`: each token names two different experts; for each client at most 48 of its tokens name any one expert, and in some clients some expert is named by exactly 48 tokens.
All inputs are finite; a program needn't handle non-finite values.
Results may differ from a plain program's by a relative error of at most 0.015.
Values may be sent and summed in bfloat16 or wider, within the bound.
A program may use at most 64 MiB of HBM per device.

v0:
```python
import jax
import jax.numpy as jnp
from jax import lax
from jax.sharding import Mesh
from jax.sharding import PartitionSpec as P

FFN = ("ffn_0", "ffn_1")


def gathered_by_axis(value, axes, dim):
    out = value
    for number in range(len(axes) - 1, -1, -1):
        out = lax.all_gather(out, axes[number], axis=dim, tiled=True)
    return out


def own_rows(terms, axes):
    running = terms.astype(jnp.bfloat16)
    for axis in axes:
        running = lax.psum_scatter(running, axis, scatter_dimension=0, tiled=True)
    return running.astype(jnp.float32)


def in_order(parts, dim):
    dims = list(parts.shape[1:])
    dims[dim] *= parts.shape[0]
    return jnp.moveaxis(parts, 0, dim).reshape(dims)


def from_everyone(value, axis):
    copies = jnp.broadcast_to(value, (lax.axis_size(axis), *value.shape))
    return lax.all_to_all(copies, axis, split_axis=0, concat_axis=0, tiled=True)


def gathered_copies(value, axis, dim):
    return in_order(from_everyone(value, axis), dim)


def of_everyone(value, axis):
    everything = from_everyone(value, axis)
    return jnp.sum(everything, axis=0)


def slot_table(routed, expert_count):
    named_hits = jnp.sum(
        (routed[:, :, None] == jnp.arange(expert_count, dtype=jnp.int32)[None, None, :]).astype(
            jnp.int32
        ),
        axis=1,
    )
    before = jnp.cumsum(named_hits, axis=0) - named_hits
    return jnp.take_along_axis(before, routed, axis=1)


def pack_rows(token_rows, routed, expert_count, capacity):
    token_count = token_rows.shape[0]
    slot_flat = routed * capacity + slot_table(routed, expert_count)
    owners = jnp.repeat(jnp.arange(token_count, dtype=jnp.int32), 2)
    source = (
        jnp.full((expert_count * capacity,), token_count, jnp.int32)
        .at[slot_flat.reshape(-1)]
        .set(owners)
    )
    padded = jnp.concatenate(
        [token_rows, jnp.zeros((1, token_rows.shape[1]), token_rows.dtype)], axis=0
    )
    return (padded[source].reshape(expert_count, capacity, token_rows.shape[1]), slot_flat)


def mix_weights(token_rows, routed, router):
    logits = jnp.dot(token_rows, router, preferred_element_type=jnp.float32)
    picked = jnp.take_along_axis(logits, routed, axis=1)
    weight_first = jax.nn.sigmoid(picked[:, 0] - picked[:, 1])
    return (weight_first, 1.0 - weight_first)


def per_device(tokens, routes, router, w_gate, w_up, w_down, adapter, upstream, bound):
    expert_count = lax.axis_size("expert")
    gathered = gathered_by_axis(tokens, FFN, 1)
    token_rows = gathered[0]
    token_count = token_rows.shape[0]
    model_width = token_rows.shape[1]
    capacity = 3 * token_count // expert_count
    routed = routes[0]
    outgoing, slot_flat = pack_rows(token_rows, routed, expert_count, capacity)
    col_count = adapter.shape[2]
    column = lax.axis_index(FFN) * col_count
    weight_first, weight_second = mix_weights(token_rows, routed, router)
    arrived = lax.all_to_all(outgoing, "expert", split_axis=0, concat_axis=0, tiled=True)
    flat_rows = arrived.reshape(-1, model_width)
    gate_out = jnp.dot(flat_rows, w_gate[0], preferred_element_type=jnp.float32)
    up_out = jnp.dot(flat_rows, w_up[0], preferred_element_type=jnp.float32)
    hidden = (jax.nn.silu(gate_out) * up_out).astype(jnp.bfloat16)
    senders = arrived.shape[0]
    slots_here = arrived.shape[1]
    down_cols = w_down[0]
    term = lax.dot_general(
        down_cols, hidden, (((0,), (1,)), ((), ())), preferred_element_type=jnp.float32
    ).astype(jnp.bfloat16)
    term = lax.optimization_barrier(term).astype(jnp.float32)
    share = own_rows(
        jnp.transpose(term.reshape(col_count * lax.axis_size(FFN), senders, slots_here), (0, 2, 1)),
        FFN,
    )
    returned = lax.all_to_all(share, "expert", split_axis=2, concat_axis=2, tiled=True)
    slot_major = jnp.transpose(returned, (0, 2, 1)).reshape(col_count, -1)
    picked = slot_major[:, slot_flat]
    mix_cols = weight_first[None, :] * picked[:, :, 0] + weight_second[None, :] * picked[:, :, 1]
    own_tokens = lax.dynamic_slice_in_dim(token_rows, column, col_count, 1)
    own_layer = (own_tokens.astype(jnp.float32) + jnp.transpose(mix_cols)).astype(jnp.bfloat16)
    layer_out = gathered_copies(own_layer, FFN, 1)
    own_cols = lax.dynamic_slice_in_dim(layer_out, column, col_count, 1)
    adapted = (
        own_cols.astype(jnp.float32)
        + jnp.dot(layer_out, adapter[0], preferred_element_type=jnp.float32)
    ).astype(jnp.bfloat16)
    grad_input = upstream[0]
    adapter_grad = lax.dot_general(
        layer_out, grad_input, (((0,), (0,)), ((), ())), preferred_element_type=jnp.float32
    )
    squared = of_everyone(jnp.sum(adapter_grad * adapter_grad), FFN)
    grad_norm = jnp.sqrt(squared)
    clip_limit = bound[0]
    factor = clip_limit / jnp.maximum(grad_norm, clip_limit)
    clipped = (adapter_grad * factor).astype(jnp.bfloat16)
    return (adapted[None], clipped[None])


def solution(mesh):
    split = Mesh(mesh.devices.reshape(mesh.shape["expert"], 8, 4), ("expert", "ffn_0", "ffn_1"))
    placed = (
        P("expert", FFN, None),
        P("expert", None, None),
        P(),
        P("expert", None, FFN),
        P("expert", None, FFN),
        P("expert", FFN, None),
        P("expert", None, FFN),
        P("expert", None, FFN),
        P("expert"),
    )
    return jax.shard_map(
        per_device,
        mesh=split,
        in_specs=placed,
        out_specs=(P("expert", None, FFN), P("expert", None, FFN)),
        check_vma=False,
    )
```

profile of v0, /device:TPU:2, one launch (start us, length us, event | category | flops | bytes accessed | tf_op | source)
XLA Modules:
  0.0 286.1 jit_solution(3763902621592552826)
XLA Ops:
  7.2 0.0 copy-start
  7.2 0.0 all-gather.2.cloned.1.call-start
  7.2 1.0 copy.48
  8.2 12.8 %all_gather.6 = bf16[1,16,4096]{2,0,1:T(2,128)(2,1)S(1)} all-gather(bf16[1,4,4096]{2,0,1:T(2,128)(2,1)S(1)} %copy.48), channel_id=1, replica_groups=mesh['expert'=8,'ffn_0'=8,'ffn_1'=4] {'ffn_1'}, dimensions={1}, use_global_device_ids=true | all-gather | bytes 163840 | tf_op jit(solution)/shard_map/all_gather | solution.py:13
  21.0 0.8 copy.49
  21.8 0.0 all-gather.2.cloned.1.call-update
  21.8 0.0 reduce-scatter.5.cloned.1.call-start
  21.8 0.8 copy.50
  22.6 0.7 convert_reduce_fusion
  23.3 0.1 copy.53
  23.4 0.1 squeeze.39
  23.6 0.1 reshape.235
  23.7 0.2 reduce_window_sum.11
  23.9 0.1 reshape.251
  24.1 1.9 gather_fusion.3
  26.0 1.4 scatter_custom_fusion
  27.5 35.2 %all-gather.2.cloned.1.call-done = bf16[1,128,4096]{2,1,0:T(8,128)(2,1)} async-done(((bf16[1,16,4096]{2,1,0:T(8,128)(2,1)}), bf16[1,128,4096]{2,1,0:T(8,128)(2,1)}) %all-gather.2.cloned.1.call-update) | async-done | bytes 1048592 | tf_op jit(solution)/shard_map/all_gather | solution.py:13
  62.7 2.3 concatenate.3
  65.0 9.7 %gather_fusion = bf16[384,4096]{1,0:T(8,128)(2,1)} fusion(bf16[129,4096]{1,0:T(8,128)(2,1)} %concatenate.3, s32[1024]{0:T(1024)S(1)} %pad_clamp_fusion.1), kind=kCustom, calls=%fused_computation | custom fusion | bytes 6292992 | tf_op jit(solution)/shard_map/gather | solution.py:67
  74.7 0.0 copy-start.5
  74.7 42.4 %all_to_all.21 = bf16[8,48,4096]{2,1,0:T(8,128)(2,1)S(1)} all-to-all(bf16[8,48,4096]{2,1,0:T(8,128)(2,1)} %bitcast.118), channel_id=1, replica_groups=mesh['expert'=8,'ffn_0'=8,'ffn_1'=4] {'expert'}, dimensions={0} | all-to-all | bytes 6291456 | tf_op jit(solution)/shard_map/all_to_all | solution.py:89
  117.1 0.0 copy-start.1
  117.1 1.7 copy-done.1
  118.8 0.0 copy-done.5
  118.8 2.6 fusion.4
  121.4 0.0 copy-done
  121.4 8.1 %fusion = bf16[4096,384]{0,1:T(8,128)(2,1)} fusion(bf16[1,384,4096]{2,1,0:T(8,128)(2,1)S(1)} %copy-done, bf16[384,4096]{1,0:T(8,128)(2,1)} %bitcast.124, bf16[1,4096,384]{2,1,0:T(8,128)(2,1)} %param.13, f32[384,384]{1,0:T(8,128)} %fusion.4), kind=kOutput, calls=%fused_computation.6 | convolution fusion | flops 2418376704 | bytes 13172736 | tf_op jit(solution)/shard_map/dot_general | solution.py:97
  129.5 0.0 copy-start.2
  129.5 0.0 reduce-scatter.5.cloned.1.call-update
  129.5 0.2 reduce-scatter.7.cloned.1.call-start
  129.8 0.1 gather.22
  129.9 44.0 %reduce-scatter.5.cloned.1.call-done = bf16[512,48,8]{0,1,2:T(8,128)(2,1)} async-done(((bf16[4096,48,8]{0,1,2:T(8,128)(2,1)}), bf16[512,48,8]{0,1,2:T(8,128)(2,1)}) %reduce-scatter.5.cloned.1.call-update) | async-done | bytes 393232 | tf_op jit(solution)/shard_map/reduce_scatter | solution.py:20
  173.9 2.7 copy.58
  176.6 2.6 reshape.259
  179.2 0.0 reduce-scatter.7.cloned.1.call-update
  179.3 0.1 reshape.229
  179.4 0.0 copy-done.2
  179.4 1.6 fusion.36
  181.0 0.0 copy-start.4
  181.0 1.4 gather_fusion.2
  182.4 0.1 reshape.238
  182.6 0.1 copy.51
  182.6 0.0 copy-done.4
  182.6 19.9 %reduce-scatter.7.cloned.1.call-done = bf16[128,384]{1,0:T(8,128)(2,1)} async-done(((bf16[512,384]{1,0:T(8,128)(2,1)}), bf16[128,384]{1,0:T(8,128)(2,1)}) %reduce-scatter.7.cloned.1.call-update) | async-done | bytes 98320
  202.5 1.1 reshape.260
  203.7 0.8 copy.59
  204.5 1.6 convert_element_type.49
  206.0 4.8 %all-to-all-start.1 = ((f32[128,48,8]{0,1,2:T(8,128)}), f32[128,48,8]{0,1,2:T(8,128)S(1)}, u32[]{:S(2)}, u32[]{:S(2)}) async-start(f32[128,48,8]{0,1,2:T(8,128)} %convert_element_type.49), calls=%async_computation.2 | async-start | bytes 393216 | tf_op jit(solution)/shard_map/all_to_all | solution.py:105
  210.8 5.3 %all-to-all-done.1 = f32[128,48,8]{0,1,2:T(8,128)S(1)} async-done(((f32[128,48,8]{0,1,2:T(8,128)}), f32[128,48,8]{0,1,2:T(8,128)S(1)}, u32[]{:S(2)}, u32[]{:S(2)}) %all-to-all-start.1) | async-done | bytes 196640 | tf_op jit(solution)/shard_map/all_to_all | solution.py:105
  216.2 0.7 gather_fusion.1
  216.9 0.0 copy-start.3
  216.9 0.9 fusion.28
  217.8 1.2 broadcast_in_dim.43
  219.0 8.4 %all-to-all-start.2 = ((bf16[32,128,128]{2,1,0:T(8,128)(2,1)}), bf16[32,128,128]{2,1,0:T(8,128)(2,1)}, u32[]{:S(2)}, u32[]{:S(2)}) async-start(bf16[32,128,128]{2,1,0:T(8,128)(2,1)} %broadcast_in_dim.43), calls=%async_computation.3 | async-start | bytes 2097152 | tf_op jit(solution)/shard_map/all_to_all | solution.py:32
  228.1 27.1 %all-to-all-done.2 = bf16[32,128,128]{2,1,0:T(8,128)(2,1)} async-done(((bf16[32,128,128]{2,1,0:T(8,128)(2,1)}), bf16[32,128,128]{2,1,0:T(8,128)(2,1)}, u32[]{:S(2)}, u32[]{:S(2)}) %all-to-all-start.2) | async-done | bytes 1048608 | tf_op jit(solution)/shard_map/all_to_all | solution.py:32
  255.2 0.0 copy-done.3
  255.2 3.8 %multiply_reduce_fusion = (f32[]{:T(128)}, f32[4096,128]{1,0:T(8,128)}) fusion(bf16[1,128,128]{2,1,0:T(8,128)(2,1)S(1)} %copy-done.3, bf16[32,128,128]{2,1,0:T(8,128)(2,1)} %all-to-all-done.2), kind=kOutput, calls=%fused_computation.13 | convolution fusion | flops 135266304 | bytes 3178500 | tf_op jit(solution)/shard_map/dot_general | solution.py:118
  259.0 1.3 broadcast_in_dim.45
  260.2 5.6 %all-to-all-start.3 = ((f32[32,1,1]{2,1,0:T(1,128)}), f32[32,1,1]{2,1,0:T(1,128)S(1)}, u32[]{:S(2)}, u32[]{:S(2)}) async-start(f32[32,1,1]{2,1,0:T(1,128)} %broadcast_in_dim.45), calls=%async_computation.4 | async-start | bytes 32768 | tf_op jit(solution)/shard_map/all_to_all | solution.py:32
  265.8 1.4 copy_bitcast_fusion
  267.2 2.3 fusion.13
  269.5 6.0 %all-to-all-done.3 = f32[32,1,1]{2,1,0:T(1,128)S(1)} async-done(((f32[32,1,1]{2,1,0:T(1,128)}), f32[32,1,1]{2,1,0:T(1,128)S(1)}, u32[]{:S(2)}, u32[]{:S(2)}) %all-to-all-start.3) | async-done | bytes 160 | tf_op jit(solution)/shard_map/all_to_all | solution.py:32
  275.5 0.6 reduce_sum.29
  276.9 2.7 fusion.14
  (11 shorter events, 0.1 us)
Async XLA Ops:
  7.2 114.2 %copy-start = (bf16[1,384,4096]{2,1,0:T(8,128)(2,1)S(1)}, bf16[1,384,4096]{2,1,0:T(8,128)(2,1)}, u32[]{:S(2)}) copy-start(bf16[1,384,4096]{2,1,0:T(8,128)(2,1)} %param.14) | copy-start | bytes 9437188
  7.2 55.5 %all-gather.2.cloned.1.call-start = ((), (), s32[]{:S(2)}) async-start(), calls=%async_computation.6 | async-start | bytes 1179648 | tf_op jit(solution)/shard_map/all_gather | solution.py:13
  21.8 152.1 %reduce-scatter.5.cloned.1.call-start = ((), (), s32[]{:S(2)}) async-start(), calls=%async_computation.7 | async-start | bytes 3538944 | tf_op jit(solution)/shard_map/reduce_scatter | solution.py:20
  74.7 44.1 %copy-start.5 = (bf16[1,4096,384]{2,1,0:T(8,128)(2,1)S(1)}, bf16[1,4096,384]{2,1,0:T(8,128)(2,1)}, u32[]{:S(2)}) copy-start(bf16[1,4096,384]{2,1,0:T(8,128)(2,1)} %param.12) | copy-start | bytes 9437188
  117.1 1.7 copy-start.1
  129.5 49.9 %copy-start.2 = (bf16[4096,8]{0,1:T(8,128)(2,1)S(1)}, bf16[4096,8]{0,1:T(8,128)(2,1)}, u32[]{:S(2)}) copy-start(bf16[4096,8]{0,1:T(8,128)(2,1)} %param.11) | copy-start | bytes 196612
  129.5 73.0 %reduce-scatter.7.cloned.1.call-start = ((), (), s32[]{:S(2)}) async-start(), calls=%async_computation.8 | async-start | bytes 491520
  181.0 1.6 copy-start.4
  206.0 10.1 %all-to-all-start.1 = ((f32[128,48,8]{0,1,2:T(8,128)}), f32[128,48,8]{0,1,2:T(8,128)S(1)}, u32[]{:S(2)}, u32[]{:S(2)}) async-start(f32[128,48,8]{0,1,2:T(8,128)} %convert_element_type.49), calls=%async_computation.2 | async-start | bytes 393216 | tf_op jit(solution)/shard_map/all_to_all | solution.py:105
  216.9 38.3 %copy-start.3 = (bf16[1,128,128]{2,1,0:T(8,128)(2,1)S(1)}, bf16[1,128,128]{2,1,0:T(8,128)(2,1)}, u32[]{:S(2)}) copy-start(bf16[1,128,128]{2,1,0:T(8,128)(2,1)} %param.16) | copy-start | bytes 98308
  219.0 36.2 %all-to-all-start.2 = ((bf16[32,128,128]{2,1,0:T(8,128)(2,1)}), bf16[32,128,128]{2,1,0:T(8,128)(2,1)}, u32[]{:S(2)}, u32[]{:S(2)}) async-start(bf16[32,128,128]{2,1,0:T(8,128)(2,1)} %broadcast_in_dim.43), calls=%async_computation.3 | async-start | bytes 2097152 | tf_op jit(solution)/shard_map/all_to_all | solution.py:32
  260.2 15.3 %all-to-all-start.3 = ((f32[32,1,1]{2,1,0:T(1,128)}), f32[32,1,1]{2,1,0:T(1,128)S(1)}, u32[]{:S(2)}, u32[]{:S(2)}) async-start(f32[32,1,1]{2,1,0:T(1,128)} %broadcast_in_dim.45), calls=%async_computation.4 | async-start | bytes 32768 | tf_op jit(solution)/shard_map/all_to_all | solution.py:32
Sparse Core Ops, SparseCore 0:
  21.9 40.6 all-gather.1
  129.6 44.1 reduce-scatter.4
  179.3 23.1 reduce-scatter.6
where the time goes:
time: 287 us; the launch traced here: 286 us
  waiting for transfers between devices  138 us (48%)
  blocking collectives  55.2 us (19%)
  local copies, waits for them, and re-layouts  33.8 us (12%)
  starting transfers between devices  19.1 us (7%)
  matrix products  18.4 us (6%)
  between operations  15.3 us (5%)
  other arithmetic  6.74 us (2%)
    reduce_scatter x1, waiting for transfers between devices, own_rows(): running = lax.psum_scatter(running, axis, scatter_dimension=0, tiled=True)  44 us
    all_to_all x1, blocking collectives, per_device(): lax.all_to_all(outgoing, 'expert', split_axis=0, concat_axis=0, tiled=True)  42.4 us
    all_gather x1, waiting for transfers between devices, gathered_by_axis(): out = lax.all_gather(out, axes[number], axis=dim, tiled=True)  35.2 us
    all_to_all x2, waiting for transfers between devices, from_everyone(): return lax.all_to_all(copies, axis, split_axis=0, concat_axis=0, tiled=True)  33.1 us
    unnamed x4, waiting for transfers between devices  19.9 us
    all_to_all x2, starting transfers between devices, from_everyone(): return lax.all_to_all(copies, axis, split_axis=0, concat_axis=0, tiled=True)  14 us
    all_gather x1, blocking collectives, gathered_by_axis(): out = lax.all_gather(out, axes[number], axis=dim, tiled=True)  12.8 us
    unnamed x18, local copies, waits for them, and re-layouts  10.7 us
  transfers between devices with their start and end apart: 6, of which 6 were waited for; matrix products, arithmetic and copies ran while one was open for 4% of the time, Pallas kernels for 0%

commit v1 on v0

--- a/solution.py
+++ b/solution.py
@@ -5,6 +5,28 @@
 from jax.sharding import PartitionSpec as P
 
 FFN = ("ffn_0", "ffn_1")
+
+
+def split_up(value, dim, length):
+    before, after = (value.shape[:dim], value.shape[dim + 1 :])
+    return jnp.moveaxis(value.reshape(*before, length, -1, *after), dim, 0)
+
+
+def laid_out(blocks, dim):
+    blocks = jnp.moveaxis(blocks, 0, dim)
+    shape = blocks.shape
+    return blocks.reshape(*shape[:dim], shape[dim] * shape[dim + 1], *shape[dim + 2 :])
+
+
+def sent_to_each(shard, axis, split_dim, concat_dim):
+    size, position = (lax.axis_size(axis), lax.axis_index(axis))
+    blocks = split_up(shard, split_dim, size)
+    done = [blocks[position]]
+    for step in range(1, size):
+        sent = blocks[(position + step) % size]
+        done.append(lax.ppermute(sent, axis, [(i, (i + step) % size) for i in range(size)]))
+    blocks = jnp.stack(done)[(position - jnp.arange(size)) % size]
+    return laid_out(blocks, concat_dim)
 
 
 def gathered_by_axis(value, axes, dim):
@@ -86,7 +108,7 @@
     col_count = adapter.shape[2]
     column = lax.axis_index(FFN) * col_count
     weight_first, weight_second = mix_weights(token_rows, routed, router)
-    arrived = lax.all_to_all(outgoing, "expert", split_axis=0, concat_axis=0, tiled=True)
+    arrived = sent_to_each(outgoing, "expert", 0, 0)
     flat_rows = arrived.reshape(-1, model_width)
     gate_out = jnp.dot(flat_rows, w_gate[0], preferred_element_type=jnp.float32)
     up_out = jnp.dot(flat_rows, w_up[0], preferred_element_type=jnp.float32)

time: 287 us -> 299 us (1.042)
  blocking collectives: 55.2 us -> 12.8 us
  waiting for transfers between devices: 138 us -> 170 us
  local copies, waits for them, and re-layouts: 33.8 us -> 44.6 us
  starting transfers between devices: 19.1 us -> 26.5 us
    all_to_all x1 -> x0, blocking collectives: 42.4 us -> none  [per_device(): lax.all_to_all(outgoing, 'expert', split_axis=0, concat_axis=0, tiled=True)]
    ppermute x0 -> x7, waiting for transfers between devices: none -> 29.5 us  [sent_to_each(): lax.ppermute(sent, axis, [(i, (i + step) % size) for i in range(size)])]
    ppermute x0 -> x7, starting transfers between devices: none -> 7.61 us  [sent_to_each(): lax.ppermute(sent, axis, [(i, (i + step) % size) for i in range(size)])]
    gather x0 -> x1, local copies, waits for them, and re-layouts: none -> 4.27 us  [sent_to_each(): blocks = jnp.stack(done)[(position - jnp.arange(size)) % size]]
    reduce_scatter x1, waiting for transfers between devices: 44 us -> 47.7 us  [own_rows(): running = lax.psum_scatter(running, axis, scatter_dimension=0, tiled=True)]
    unnamed x18 -> x20, local copies, waits for them, and re-layouts: 10.7 us -> 13.7 us
  transfers between devices with their start and end apart: 6 -> 13, of which waited for: 6 -> 9; matrix products, arithmetic and copies ran while one was open for 4% -> 6% of each run, Pallas kernels for 0% -> 0%
where the time goes in v1:
time: 299 us; the launch traced here: 298 us
  waiting for transfers between devices  170 us (57%)
  local copies, waits for them, and re-layouts  44.6 us (15%)
  starting transfers between devices  26.5 us (9%)
  matrix products  21.2 us (7%)
  between operations  15.5 us (5%)
  blocking collectives  12.8 us (4%)
  other arithmetic  6.76 us (2%)
    reduce_scatter x1, waiting for transfers between devices, own_rows(): running = lax.psum_scatter(running, axis, scatter_dimension=0, tiled=True)  47.7 us
    all_gather x1, waiting for transfers between devices, gathered_by_axis(): out = lax.all_gather(out, axes[number], axis=dim, tiled=True)  35 us
    all_to_all x2, waiting for transfers between devices, from_everyone(): return lax.all_to_all(copies, axis, split_axis=0, concat_axis=0, tiled=True)  33.1 us
    ppermute x7, waiting for transfers between devices, sent_to_each(): lax.ppermute(sent, axis, [(i, (i + step) % size) for i in range(size)])  29.5 us
    unnamed x4, waiting for transfers between devices  19.8 us
    all_to_all x2, starting transfers between devices, from_everyone(): return lax.all_to_all(copies, axis, split_axis=0, concat_axis=0, tiled=True)  14 us
    unnamed x20, local copies, waits for them, and re-layouts  13.7 us
    all_gather x1, blocking collectives, gathered_by_axis(): out = lax.all_gather(out, axes[number], axis=dim, tiled=True)  12.8 us
  transfers between devices with their start and end apart: 13, of which 9 were waited for; matrix products, arithmetic and copies ran while one was open for 6% of the time, Pallas kernels for 0%

profile of v1, /device:TPU:2, one launch (start us, length us, event | category | flops | bytes accessed | tf_op | source)
XLA Modules:
  0.0 297.8 jit_solution(648970934692313867)
XLA Ops:
  7.2 1.0 copy.48
  8.2 12.8 %all_gather.6 = bf16[1,16,4096]{2,0,1:T(2,128)(2,1)S(1)} all-gather(bf16[1,4,4096]{2,0,1:T(2,128)(2,1)S(1)} %copy.48), channel_id=1, replica_groups=mesh['expert'=8,'ffn_0'=8,'ffn_1'=4] {'ffn_1'}, dimensions={1}, use_global_device_ids=true | all-gather | bytes 163840 | tf_op jit(solution)/shard_map/all_gather | solution.py:35
  21.0 0.8 copy.49
  21.8 0.0 reduce-scatter.5.cloned.1.call-start
  21.9 0.8 copy.50
  22.7 0.7 convert_reduce_fusion
  23.4 0.1 copy.53
  23.5 0.1 squeeze.60
  23.7 0.1 reshape.286
  23.8 0.2 reduce_window_sum.11
  24.0 0.1 reshape.302
  24.2 1.9 gather_fusion.4
  26.2 1.4 scatter_custom_fusion
  27.6 35.0 %all-gather.2.cloned.1.call-done = bf16[1,128,4096]{2,1,0:T(8,128)(2,1)} async-done(((bf16[1,16,4096]{2,1,0:T(8,128)(2,1)}), bf16[1,128,4096]{2,1,0:T(8,128)(2,1)}) %all-gather.2.cloned.1.call-update) | async-done | bytes 1048592 | tf_op jit(solution)/shard_map/all_gather | solution.py:35
  62.7 2.4 concatenate.3
  65.0 9.6 %gather_fusion = bf16[384,4096]{1,0:T(8,128)(2,1)} fusion(bf16[129,4096]{1,0:T(8,128)(2,1)} %concatenate.3, s32[1024]{0:T(1024)S(1)} %pad_clamp_fusion.2), kind=kCustom, calls=%fused_computation | custom fusion | bytes 6292992 | tf_op jit(solution)/shard_map/gather | solution.py:89
  74.6 2.8 dynamic-slice_bitcast_fusion
  77.5 1.8 collective-permute-start.6
  79.2 1.8 collective-permute-start.5
  81.0 0.1 collective-permute-start.4
  81.1 1.5 collective-permute-start.3
  82.6 2.6 collective-permute-done
  85.2 1.5 collective-permute-start.1
  86.6 0.8 bitcast_dynamic-update-slice_fusion.6
  87.4 18.3 %collective-permute-done.1 = bf16[1,48,4096]{2,1,0:T(8,128)(2,1)S(1)} collective-permute-done((bf16[1,48,4096]{2,1,0:T(8,128)(2,1)S(1)}, bf16[1,48,4096]{2,1,0:T(8,128)(2,1)S(1)}, u32[]{:S(2)}, u32[]{:S(2)}) %collective-permute-start.1) | collective-permute-done | bytes 393248 | tf_op jit(solution)/shard_map/ppermute | solution.py:27
  105.8 1.0 collective-permute-start.2
  106.8 0.8 bitcast_dynamic-update-slice_fusion.5
  107.6 8.5 %collective-permute-done.2 = bf16[1,48,4096]{2,1,0:T(8,128)(2,1)S(1)} collective-permute-done((bf16[1,48,4096]{2,1,0:T(8,128)(2,1)S(1)}, bf16[1,48,4096]{2,1,0:T(8,128)(2,1)S(1)}, u32[]{:S(2)}, u32[]{:S(2)}) %collective-permute-start.2) | collective-permute-done | bytes 393248 | tf_op jit(solution)/shard_map/ppermute | solution.py:27
  116.1 0.8 bitcast_dynamic-update-slice_fusion.4
  116.9 0.8 bitcast_dynamic-update-slice_fusion.3
  117.7 0.8 bitcast_dynamic-update-slice_fusion.2
  118.4 0.8 bitcast_dynamic-update-slice_fusion.1
  119.2 0.8 bitcast_dynamic-update-slice_fusion
  120.0 4.3 %gather_fusion.1 = bf16[8,48,4096]{2,1,0:T(8,128)(2,1)} fusion(bf16[8,48,4096]{2,1,0:T(8,128)(2,1)} %bitcast.22, s32[1024]{0:T(1024)S(1)} %pad_clamp_fusion.1), kind=kCustom, calls=%fused_computation.1 | custom fusion | bytes 6291488 | tf_op jit(solution)/shard_map/gather | solution.py:28
  124.3 5.4 %fusion.4 = f32[384,384]{1,0:T(8,128)} fusion(bf16[384,4096]{1,0:T(8,128)(2,1)} %bitcast.154, bf16[1,4096,384]{2,1,0:T(8,128)(2,1)} %param.12), kind=kOutput, calls=%fused_computation.11 | convolution fusion | flops 1207959552 | bytes 6881280 | tf_op jit(solution)/shard_map/dot_general | solution.py:113
  129.7 8.1 %fusion = bf16[4096,384]{0,1:T(8,128)(2,1)} fusion(bf16[1,384,4096]{2,1,0:T(8,128)(2,1)S(1)} %copy-done, bf16[384,4096]{1,0:T(8,128)(2,1)} %bitcast.155, bf16[1,4096,384]{2,1,0:T(8,128)(2,1)} %param.13, f32[384,384]{1,0:T(8,128)} %fusion.4), kind=kOutput, calls=%fused_computation.7 | convolution fusion | flops 2418376704 | bytes 13172736 | tf_op jit(solution)/shard_map/dot_general | solution.py:119
  137.9 0.1 gather.26
  138.0 47.7 %reduce-scatter.5.cloned.1.call-done = bf16[512,48,8]{0,1,2:T(8,128)(2,1)} async-done(((bf16[4096,48,8]{0,1,2:T(8,128)(2,1)}), bf16[512,48,8]{0,1,2:T(8,128)(2,1)}) %reduce-scatter.5.cloned.1.call-update) | async-done | bytes 393232 | tf_op jit(solution)/shard_map/reduce_scatter | solution.py:42
  185.7 2.7 copy.58
  188.4 2.6 reshape.311
  191.1 0.1 reshape.280
  191.2 1.6 fusion.38
  192.8 1.4 gather_fusion.3
  194.2 0.1 reshape.289
  194.4 0.1 copy.51
  194.4 19.8 %reduce-scatter.7.cloned.1.call-done = bf16[128,384]{1,0:T(8,128)(2,1)} async-done(((bf16[512,384]{1,0:T(8,128)(2,1)}), bf16[128,384]{1,0:T(8,128)(2,1)}) %reduce-scatter.7.cloned.1.call-update) | async-done | bytes 98320
  214.2 1.1 reshape.312
  215.4 0.8 copy.59
  216.2 1.6 convert_element_type.49
  217.8 4.8 %all-to-all-start = ((f32[128,48,8]{0,1,2:T(8,128)}), f32[128,48,8]{0,1,2:T(8,128)S(1)}, u32[]{:S(2)}, u32[]{:S(2)}) async-start(f32[128,48,8]{0,1,2:T(8,128)} %convert_element_type.49), calls=%async_computation.1 | async-start | bytes 393216 | tf_op jit(solution)/shard_map/all_to_all | solution.py:127
  222.6 5.3 %all-to-all-done = f32[128,48,8]{0,1,2:T(8,128)S(1)} async-done(((f32[128,48,8]{0,1,2:T(8,128)}), f32[128,48,8]{0,1,2:T(8,128)S(1)}, u32[]{:S(2)}, u32[]{:S(2)}) %all-to-all-start) | async-done | bytes 196640 | tf_op jit(solution)/shard_map/all_to_all | solution.py:127
  227.9 0.7 gather_fusion.2
  228.7 0.9 fusion.28
  229.5 1.2 broadcast_in_dim.44
  230.8 8.4 %all-to-all-start.1 = ((bf16[32,128,128]{2,1,0:T(8,128)(2,1)}), bf16[32,128,128]{2,1,0:T(8,128)(2,1)}, u32[]{:S(2)}, u32[]{:S(2)}) async-start(bf16[32,128,128]{2,1,0:T(8,128)(2,1)} %broadcast_in_dim.44), calls=%async_computation.2 | async-start | bytes 2097152 | tf_op jit(solution)/shard_map/all_to_all | solution.py:54
  239.8 27.1 %all-to-all-done.1 = bf16[32,128,128]{2,1,0:T(8,128)(2,1)} async-done(((bf16[32,128,128]{2,1,0:T(8,128)(2,1)}), bf16[32,128,128]{2,1,0:T(8,128)(2,1)}, u32[]{:S(2)}, u32[]{:S(2)}) %all-to-all-start.1) | async-done | bytes 1048608 | tf_op jit(solution)/shard_map/all_to_all | solution.py:54
  266.9 3.8 %multiply_reduce_fusion = (f32[]{:T(128)}, f32[4096,128]{1,0:T(8,128)}) fusion(bf16[1,128,128]{2,1,0:T(8,128)(2,1)S(1)} %copy-done.2, bf16[32,128,128]{2,1,0:T(8,128)(2,1)} %all-to-all-done.1), kind=kOutput, calls=%fused_computation.14 | convolution fusion | flops 135266304 | bytes 3178500 | tf_op jit(solution)/shard_map/dot_general | solution.py:140
  270.7 1.3 broadcast_in_dim.46
  272.0 5.6 %all-to-all-start.2 = ((f32[32,1,1]{2,1,0:T(1,128)}), f32[32,1,1]{2,1,0:T(1,128)S(1)}, u32[]{:S(2)}, u32[]{:S(2)}) async-start(f32[32,1,1]{2,1,0:T(1,128)} %broadcast_in_dim.46), calls=%async_computation.3 | async-start | bytes 32768 | tf_op jit(solution)/shard_map/all_to_all | solution.py:54
  277.6 1.4 copy_bitcast_fusion
  279.0 2.3 fusion.13
  281.2 6.0 %all-to-all-done.2 = f32[32,1,1]{2,1,0:T(1,128)S(1)} async-done(((f32[32,1,1]{2,1,0:T(1,128)}), f32[32,1,1]{2,1,0:T(1,128)S(1)}, u32[]{:S(2)}, u32[]{:S(2)}) %all-to-all-start.2) | async-done | bytes 160 | tf_op jit(solution)/shard_map/all_to_all | solution.py:54
  287.3 0.6 reduce_sum.29
  288.6 2.7 fusion.14
  (31 shorter events, 0.3 us)
Async XLA Ops:
  7.2 122.6 %copy-start = (bf16[1,384,4096]{2,1,0:T(8,128)(2,1)S(1)}, bf16[1,384,4096]{2,1,0:T(8,128)(2,1)}, u32[]{:S(2)}) copy-start(bf16[1,384,4096]{2,1,0:T(8,128)(2,1)} %param.14) | copy-start | bytes 9437188
  7.2 55.5 %all-gather.2.cloned.1.call-start = ((), (), s32[]{:S(2)}) async-start(), calls=%async_computation.5 | async-start | bytes 1179648 | tf_op jit(solution)/shard_map/all_gather | solution.py:35
  21.8 163.9 %reduce-scatter.5.cloned.1.call-start = ((), (), s32[]{:S(2)}) async-start(), calls=%async_computation.6 | async-start | bytes 3538944 | tf_op jit(solution)/shard_map/reduce_scatter | solution.py:42
  77.4 7.7 %collective-permute-start = (bf16[1,48,4096]{2,1,0:T(8,128)(2,1)S(1)}, bf16[1,48,4096]{2,1,0:T(8,128)(2,1)S(1)}, u32[]{:S(2)}, u32[]{:S(2)}) collective-permute-start(bf16[1,48,4096]{2,1,0:T(8,128)(2,1)S(1)} %get-tuple-element.10), channel_id=1, source_target_pairs={{0,32},{32,64},{64,96},{96,128},{128,160},{160,192},{192,224},{224... | collective-permute-start | bytes 1179656 | tf_op jit(solution)/shard_map/ppermute | solution.py:27
  77.5 41.8 %collective-permute-start.6 = (bf16[1,48,4096]{2,1,0:T(8,128)(2,1)S(1)}, bf16[1,48,4096]{2,1,0:T(8,128)(2,1)S(1)}, u32[]{:S(2)}, u32[]{:S(2)}) collective-permute-start(bf16[1,48,4096]{2,1,0:T(8,128)(2,1)S(1)} %get-tuple-element.4), channel_id=1, source_target_pairs={{0,224},{32,0},{64,32},{96,64},{128,96},{160,128},{192,160},{224,1... | collective-permute-start | bytes 1179656 | tf_op jit(solution)/shard_map/ppermute | solution.py:27
  79.2 39.2 %collective-permute-start.5 = (bf16[1,48,4096]{2,1,0:T(8,128)(2,1)S(1)}, bf16[1,48,4096]{2,1,0:T(8,128)(2,1)S(1)}, u32[]{:S(2)}, u32[]{:S(2)}) collective-permute-start(bf16[1,48,4096]{2,1,0:T(8,128)(2,1)S(1)} %get-tuple-element.5), channel_id=1, source_target_pairs={{0,192},{32,224},{64,0},{96,32},{128,64},{160,96},{192,128},{224,1... | collective-permute-start | bytes 1179656 | tf_op jit(solution)/shard_map/ppermute | solution.py:27
  81.0 36.7 %collective-permute-start.4 = (bf16[1,48,4096]{2,1,0:T(8,128)(2,1)S(1)}, bf16[1,48,4096]{2,1,0:T(8,128)(2,1)S(1)}, u32[]{:S(2)}, u32[]{:S(2)}) collective-permute-start(bf16[1,48,4096]{2,1,0:T(8,128)(2,1)S(1)} %get-tuple-element.6), channel_id=1, source_target_pairs={{0,160},{32,192},{64,224},{96,0},{128,32},{160,64},{192,96},{224,1... | collective-permute-start | bytes 1179656 | tf_op jit(solution)/shard_map/ppermute | solution.py:27
  81.1 35.7 %collective-permute-start.3 = (bf16[1,48,4096]{2,1,0:T(8,128)(2,1)S(1)}, bf16[1,48,4096]{2,1,0:T(8,128)(2,1)S(1)}, u32[]{:S(2)}, u32[]{:S(2)}) collective-permute-start(bf16[1,48,4096]{2,1,0:T(8,128)(2,1)S(1)} %get-tuple-element.7), channel_id=1, source_target_pairs={{0,128},{32,160},{64,192},{96,224},{128,0},{160,32},{192,64},{224,... | collective-permute-start | bytes 1179656 | tf_op jit(solution)/shard_map/ppermute | solution.py:27
  85.2 20.6 %collective-permute-start.1 = (bf16[1,48,4096]{2,1,0:T(8,128)(2,1)S(1)}, bf16[1,48,4096]{2,1,0:T(8,128)(2,1)S(1)}, u32[]{:S(2)}, u32[]{:S(2)}) collective-permute-start(bf16[1,48,4096]{2,1,0:T(8,128)(2,1)S(1)} %get-tuple-element.9), channel_id=1, source_target_pairs={{0,64},{32,96},{64,128},{96,160},{128,192},{160,224},{192,0},{224,... | collective-permute-start | bytes 1179656 | tf_op jit(solution)/shard_map/ppermute | solution.py:27
  105.8 10.3 %collective-permute-start.2 = (bf16[1,48,4096]{2,1,0:T(8,128)(2,1)S(1)}, bf16[1,48,4096]{2,1,0:T(8,128)(2,1)S(1)}, u32[]{:S(2)}, u32[]{:S(2)}) collective-permute-start(bf16[1,48,4096]{2,1,0:T(8,128)(2,1)S(1)} %get-tuple-element.8), channel_id=1, source_target_pairs={{0,96},{32,128},{64,160},{96,192},{128,224},{160,0},{192,32},{224,... | collective-permute-start | bytes 1179656 | tf_op jit(solution)/shard_map/ppermute | solution.py:27
  137.8 53.4 %copy-start.1 = (bf16[4096,8]{0,1:T(8,128)(2,1)S(1)}, bf16[4096,8]{0,1:T(8,128)(2,1)}, u32[]{:S(2)}) copy-start(bf16[4096,8]{0,1:T(8,128)(2,1)} %param.11) | copy-start | bytes 196612
  137.8 76.4 %reduce-scatter.7.cloned.1.call-start = ((), (), s32[]{:S(2)}) async-start(), calls=%async_computation.7 | async-start | bytes 491520
  192.8 1.6 copy-start.3
  217.8 10.2 %all-to-all-start = ((f32[128,48,8]{0,1,2:T(8,128)}), f32[128,48,8]{0,1,2:T(8,128)S(1)}, u32[]{:S(2)}, u32[]{:S(2)}) async-start(f32[128,48,8]{0,1,2:T(8,128)} %convert_element_type.49), calls=%async_computation.1 | async-start | bytes 393216 | tf_op jit(solution)/shard_map/all_to_all | solution.py:127
  228.6 38.3 %copy-start.2 = (bf16[1,128,128]{2,1,0:T(8,128)(2,1)S(1)}, bf16[1,128,128]{2,1,0:T(8,128)(2,1)}, u32[]{:S(2)}) copy-start(bf16[1,128,128]{2,1,0:T(8,128)(2,1)} %param.16) | copy-start | bytes 98308
  230.8 36.2 %all-to-all-start.1 = ((bf16[32,128,128]{2,1,0:T(8,128)(2,1)}), bf16[32,128,128]{2,1,0:T(8,128)(2,1)}, u32[]{:S(2)}, u32[]{:S(2)}) async-start(bf16[32,128,128]{2,1,0:T(8,128)(2,1)} %broadcast_in_dim.44), calls=%async_computation.2 | async-start | bytes 2097152 | tf_op jit(solution)/shard_map/all_to_all | solution.py:54
  272.0 15.3 %all-to-all-start.2 = ((f32[32,1,1]{2,1,0:T(1,128)}), f32[32,1,1]{2,1,0:T(1,128)S(1)}, u32[]{:S(2)}, u32[]{:S(2)}) async-start(f32[32,1,1]{2,1,0:T(1,128)} %broadcast_in_dim.46), calls=%async_computation.3 | async-start | bytes 32768 | tf_op jit(solution)/shard_map/all_to_all | solution.py:54
Sparse Core Ops, SparseCore 0:
  21.9 40.6 all-gather.1
  137.9 47.6 reduce-scatter.4
  191.1 23.0 reduce-scatter.6
